TPU v7x, 32 devices: a whole 2x2x4 slice. The times are simulated.
32 devices in a mesh: rp: 2 (over x), pb: 16 (over z, y, core).
Axes of the slice: x: 2, y: 2, z: 4, core: 2. Of those that a mesh axis runs over, the one named last changes fastest.
Arguments:
- wannier_g: bfloat16 [2, 1024, 32, 1152], P(None, 'rp', 'pb'), may hold values from -0.19921875 to 0.19921875
- rp_coords: int32 [3, 1024], replicated, may hold values from -8 to 8
- q_coords: int32 [3, 64], P(None, ('rp', 'pb')), may hold values from 0 to 15
- k_index: int32 [1], replicated, may hold values from 0 to 7
- k_vectors: bfloat16 [8, 2, 32, 32], replicated, may hold values from -0.75 to 0.75
- kq_vectors: bfloat16 [64, 2, 32, 32], P(('rp', 'pb')), may hold values from -0.75 to 0.75
- modes: bfloat16 [64, 2, 36, 36], P(('rp', 'pb')), may hold values from -0.75 to 0.75
Outputs:
- rotated: float32 [64, 2, 32, 1152], P(('rp', 'pb'))
All inputs are finite; a program needn't handle non-finite values.
Results may differ from a plain program's by a relative error of at most 0.0054.
Values may be sent and summed in bfloat16 or wider, within the bound.
A program may use at most 64 MiB of HBM per device.

v0:
```python
import math
import jax
import jax.numpy as jnp
from jax import lax
from jax.sharding import PartitionSpec as P

NK = 16


def phases(q_rows, r_coords):
    turns = jnp.mod(jnp.sum(q_rows[:, :, None] * r_coords[:, None, :], axis=0), NK)
    angle = turns.astype(jnp.float32) * (2.0 * math.pi / NK)
    cosine = jnp.cos(angle).astype(jnp.bfloat16)
    sine = jnp.sin(angle).astype(jnp.bfloat16)
    return (jnp.concatenate([cosine, -sine], axis=1), jnp.concatenate([sine, cosine], axis=1))


def rotate(fourier, mode_vecs, unit, kq_vecs):
    count = fourier.shape[0]
    bands = kq_vecs.shape[2]
    branches = mode_vecs.shape[2]
    field = fourier.reshape(count, 2, bands, bands, branches)
    e_real, e_imag = (mode_vecs[:, 0], mode_vecs[:, 1])
    e_block = jnp.stack([jnp.stack([e_real, e_imag], 2), jnp.stack([-e_imag, e_real], 2)], 1)
    by_mode = jnp.einsum(
        "qcmnv,qcvdu->qdmnu", field, e_block, preferred_element_type=jnp.float32
    ).astype(jnp.bfloat16)
    u_real, u_imag = (unit[0], unit[1])
    u_block = jnp.stack([jnp.stack([u_real, u_imag], 1), jnp.stack([-u_imag, u_real], 1)], 0)
    by_band = jnp.einsum(
        "qcmnu,cndj->qdmju", by_mode, u_block, preferred_element_type=jnp.float32
    ).astype(jnp.bfloat16)
    v_real, v_imag = (kq_vecs[:, 0], kq_vecs[:, 1])
    v_block = jnp.stack([jnp.stack([v_real, -v_imag], 2), jnp.stack([v_imag, v_real], 2)], 1)
    result = jnp.einsum("qcmju,qcmdi->qdiju", by_band, v_block, preferred_element_type=jnp.float32)
    return result.reshape(count, 2, bands, bands * branches)


def body(wannier_g, rp_coords, q_coords, k_index, k_vectors, kq_vectors, modes):
    q_all = lax.all_gather(q_coords, ("rp", "pb"), axis=1, tiled=True)
    total = q_all.shape[1]
    groups = lax.axis_size("rp")
    block = total // groups
    local = wannier_g.shape[1]
    own_coords = lax.dynamic_slice_in_dim(rp_coords, lax.axis_index("rp") * local, local, 1)
    right = wannier_g.reshape(2 * local, -1)
    left_real, left_imag = phases(q_all, own_coords)
    f_real = jnp.dot(left_real, right, preferred_element_type=jnp.float32)
    f_imag = jnp.dot(left_imag, right, preferred_element_type=jnp.float32)
    summed = lax.psum_scatter(jnp.stack([f_real, f_imag], 1), "rp", scatter_dimension=0, tiled=True)
    fourier = summed.astype(jnp.bfloat16).reshape(block, 2, wannier_g.shape[2], wannier_g.shape[3])
    owned = lax.all_to_all(fourier, "pb", split_axis=0, concat_axis=2, tiled=True)
    select = (jnp.arange(k_vectors.shape[0]) == k_index[0]).astype(jnp.bfloat16)
    unit = jnp.einsum("k,kcnj->cnj", select, k_vectors, preferred_element_type=jnp.float32).astype(
        jnp.bfloat16
    )
    return rotate(owned, modes, unit, kq_vectors)


def solution(mesh):
    return jax.shard_map(
        body,
        mesh=mesh,
        in_specs=(
            P(None, "rp", "pb", None),
            P(),
            P(None, ("rp", "pb")),
            P(),
            P(),
            P(("rp", "pb"), None, None, None),
            P(("rp", "pb"), None, None, None),
        ),
        out_specs=P(("rp", "pb"), None, None, None),
        check_vma=False,
    )
```

profile of v0, /device:TPU:0, one launch (start us, length us, event | category | flops | bytes accessed | tf_op | source)
XLA Modules:
  0.0 110.1 jit_solution(14693091623832037747)
XLA Ops:
  6.5 43.7 %all-gather = s32[32,2,3]{2,1,0:T(2,128)S(1)} all-gather(s32[1,2,3]{2,1,0:T(2,128)} %bitcast.115), channel_id=1, replica_groups=mesh['rp'=2,'pb'=16] {'rp','pb'}, dimensions={0}, use_global_device_ids=true | all-gather | bytes 792 | tf_op jit(solution)/shard_map/all_gather | solution.py:40
  50.3 0.7 constant_dynamic-slice_fusion
  51.0 0.1 multiply_reduce_fusion
  51.1 0.5 fusion.32
  51.6 0.5 cosine_convert_fusion
  52.1 3.2 %copy.104 = bf16[128,8,2,1152]{3,1,2,0:T(8,128)(2,1)S(1)} copy(bf16[128,8,2,1152]{3,2,1,0:T(2,128)(2,1)} %bitcast.107) | data formatting | bytes 9437184
  55.3 0.9 convolution_bitcast_fusion.1
  56.2 0.9 convolution_bitcast_fusion
  57.2 1.1 pad_maximum_fusion
  59.1 0.2 fusion.15
  59.6 17.1 %reduce-scatter.2.cloned.1.call-done = f32[32,2,2304]{2,0,1:T(8,128)} async-done(((f32[64,2,2304]{2,0,1:T(8,128)}), f32[32,2,2304]{2,0,1:T(8,128)}) %reduce-scatter.2.cloned.1.call-update) | async-done | bytes 589840 | tf_op jit(solution)/shard_map/reduce_scatter | solution.py:50
  76.7 1.1 convert_element_type.32
  77.8 0.9 copy.77
  78.7 5.6 %all-to-all-start = ((bf16[32,2,2,1152]{3,2,1,0:T(2,128)(2,1)}), bf16[32,2,2,1152]{3,2,1,0:T(2,128)(2,1)S(1)}, u32[]{:S(2)}, u32[]{:S(2)}) async-start(bf16[32,2,2,1152]{3,2,1,0:T(2,128)(2,1)} %copy.77), calls=%async_computation.1 | async-start | bytes 589824 | tf_op jit(solution)/shard_map/all_to_all | solution.py:52
  84.4 0.1 maximum_bitcast_fusion.3
  84.5 0.1 maximum_bitcast_fusion
  84.7 10.2 %all-to-all-done = bf16[32,2,2,1152]{3,2,1,0:T(2,128)(2,1)S(1)} async-done(((bf16[32,2,2,1152]{3,2,1,0:T(2,128)(2,1)}), bf16[32,2,2,1152]{3,2,1,0:T(2,128)(2,1)S(1)}, u32[]{:S(2)}, u32[]{:S(2)}) %all-to-all-start) | async-done | bytes 294944 | tf_op jit(solution)/shard_map/all_to_all | solution.py:52
  94.9 0.2 copy.97
  95.1 3.0 %reshape.54 = bf16[2,2,32,32,36,1]{4,3,1,2,0,5:T(8,128)(2,1)S(1)} reshape(bf16[2,2,16,2,1152]{4,1,3,2,0:T(2,128)(2,1)S(1)} %copy.97) | data formatting | bytes 589824 | tf_op jit(solution)/shard_map/reshape | solution.py:22
  98.1 0.5 fusion
  98.6 0.5 fusion.1
  99.1 0.5 convolution_bitcast_fusion.2
  99.6 1.2 %copy.83 = f32[2,2,32,32,36]{4,3,2,1,0:T(8,128)S(1)} copy(f32[2,2,32,32,36]{4,2,3,1,0:T(8,128)S(1)} %convolution_bitcast_fusion.2) | data formatting | bytes 1179648 | tf_op jit(solution)/shard_map/qcmju,qcmdi->qdiju/dot_general | solution.py:35
  100.8 2.4 %reshape.48 = f32[2,2,32,1152]{3,2,1,0:T(8,128)} reshape(f32[2,2,32,32,36]{4,3,2,1,0:T(8,128)S(1)} %copy.83) | data formatting | bytes 1179648 | tf_op jit(solution)/shard_map/reshape | solution.py:36
  (22 shorter events, 0.6 us)
Async XLA Ops:
  6.5 52.5 %copy-start = (bf16[8,2,32,32]{3,2,1,0:T(8,128)(2,1)S(1)}, bf16[8,2,32,32]{3,2,1,0:T(8,128)(2,1)}, u32[]{:S(2)}) copy-start(bf16[8,2,32,32]{3,2,1,0:T(8,128)(2,1)} %param.11) | copy-start | bytes 98308
  6.5 70.1 %reduce-scatter.2.cloned.1.call-start = ((), (), s32[]{:S(2)}) async-start(), calls=%async_computation.2 | async-start | bytes 1769472 | tf_op jit(solution)/shard_map/reduce_scatter | solution.py:50
  57.1 1.1 %copy-start.1 = (bf16[2,2,36,36]{3,1,2,0:T(2,128)(2,1)S(1)}, bf16[2,2,36,36]{3,1,2,0:T(2,128)(2,1)}, u32[]{:S(2)}) copy-start(bf16[2,2,36,36]{3,1,2,0:T(2,128)(2,1)} %param.13) | copy-start | bytes 31108
  57.2 2.2 %copy-start.2 = (bf16[2,2,32,32]{3,2,1,0:T(8,128)(2,1)S(1)}, bf16[2,2,32,32]{3,2,1,0:T(8,128)(2,1)}, u32[]{:S(2)}) copy-start(bf16[2,2,32,32]{3,2,1,0:T(8,128)(2,1)} %param.12) | copy-start | bytes 24580
  78.7 16.2 %all-to-all-start = ((bf16[32,2,2,1152]{3,2,1,0:T(2,128)(2,1)}), bf16[32,2,2,1152]{3,2,1,0:T(2,128)(2,1)S(1)}, u32[]{:S(2)}, u32[]{:S(2)}) async-start(bf16[32,2,2,1152]{3,2,1,0:T(2,128)(2,1)} %copy.77), calls=%async_computation.1 | async-start | bytes 589824 | tf_op jit(solution)/shard_map/all_to_all | solution.py:52
Sparse Core Ops, SparseCore 0:
  58.4 18.1 reduce-scatter.1
where the time goes:
time: 110 us
  blocking collectives  43.7 us (40%)
  waiting for transfers between devices  27.3 us (25%)
  between operations  14.3 us (13%)
  local copies, waits for them, and re-layouts  12.2 us (11%)
  starting transfers between devices  5.61 us (5%)
  other arithmetic  3.58 us (3%)
  matrix products  3.51 us (3%)
    all_gather x1, blocking collectives, body(): q_all = lax.all_gather(q_coords, ('rp', 'pb'), axis=1, tiled=True)  43.7 us
    reduce_scatter x1, waiting for transfers between devices, body(): lax.psum_scatter(jnp.stack([f_real, f_imag], 1), 'rp', scatter_dimension=...  17.1 us
    all_to_all x1, waiting for transfers between devices, body(): lax.all_to_all(fourier, 'pb', split_axis=0, concat_axis=2, tiled=True)  10.2 us
    all_to_all x1, starting transfers between devices, body(): lax.all_to_all(fourier, 'pb', split_axis=0, concat_axis=2, tiled=True)  5.61 us
    unnamed x11, local copies, waits for them, and re-layouts  3.46 us
    reshape x2, local copies, waits for them, and re-layouts, rotate(): field = fourier.reshape(count, 2, bands, bands, branches)  3.2 us
    reshape x1, local copies, waits for them, and re-layouts, rotate(): return result.reshape(count, 2, bands, bands * branches)  2.44 us
  transfers between devices with their start and end apart: 2, of which 2 were waited for; matrix products, arithmetic and copies ran while one was open for 1% of the time, Pallas kernels for 0%

commit v1 on v0

--- a/solution.py
+++ b/solution.py
@@ -37,7 +37,7 @@
 
 
 def body(wannier_g, rp_coords, q_coords, k_index, k_vectors, kq_vectors, modes):
-    q_all = lax.all_gather(q_coords, ("rp", "pb"), axis=1, tiled=True)
+    q_all = jnp.concatenate(lax.all_gather(q_coords, ("rp", "pb")), axis=1)
     total = q_all.shape[1]
     groups = lax.axis_size("rp")
     block = total // groups

time: 110 us -> 110 us (level)
    unnamed x11 -> x10, local copies, waits for them, and re-layouts: 3.46 us -> 3.39 us
where the time goes in v1:
time: 110 us
  blocking collectives  43.7 us (40%)
  waiting for transfers between devices  27.3 us (25%)
  between operations  14.3 us (13%)
  local copies, waits for them, and re-layouts  12.2 us (11%)
  starting transfers between devices  5.61 us (5%)
  other arithmetic  3.58 us (3%)
  matrix products  3.51 us (3%)
    all_gather x1, blocking collectives, body(): q_all = jnp.concatenate(lax.all_gather(q_coords, ('rp', 'pb')), axis=1)  43.7 us
    reduce_scatter x1, waiting for transfers between devices, body(): lax.psum_scatter(jnp.stack([f_real, f_imag], 1), 'rp', scatter_dimension=...  17.1 us
    all_to_all x1, waiting for transfers between devices, body(): lax.all_to_all(fourier, 'pb', split_axis=0, concat_axis=2, tiled=True)  10.2 us
    all_to_all x1, starting transfers between devices, body(): lax.all_to_all(fourier, 'pb', split_axis=0, concat_axis=2, tiled=True)  5.61 us
    unnamed x10, local copies, waits for them, and re-layouts  3.39 us
    reshape x2, local copies, waits for them, and re-layouts, rotate(): field = fourier.reshape(count, 2, bands, bands, branches)  3.2 us
    reshape x1, local copies, waits for them, and re-layouts, rotate(): return result.reshape(count, 2, bands, bands * branches)  2.44 us
  transfers between devices with their start and end apart: 2, of which 2 were waited for; matrix products, arithmetic and copies ran while one was open for 1% of the time, Pallas kernels for 0%

profile of v1, /device:TPU:0, one launch (start us, length us, event | category | flops | bytes accessed | tf_op | source)
XLA Modules:
  0.0 110.1 jit_solution(14693091623832037747)
XLA Ops:
  6.5 43.7 %all-gather.1 = s32[32,3,2]{1,2,0:T(2,128)S(1)} all-gather(s32[1,3,2]{1,2,0:T(2,128)} %bitcast.113), channel_id=2, replica_groups=mesh['rp'=2,'pb'=16] {'rp','pb'}, dimensions={0}, use_global_device_ids=true | all-gather | bytes 792 | tf_op jit(solution)/shard_map/all_gather | solution.py:40
  50.3 0.7 constant_dynamic-slice_fusion
  51.0 0.1 multiply_reduce_fusion
  51.1 0.5 fusion.32
  51.6 0.5 cosine_convert_fusion
  52.1 3.2 %copy.104 = bf16[128,8,2,1152]{3,1,2,0:T(8,128)(2,1)S(1)} copy(bf16[128,8,2,1152]{3,2,1,0:T(2,128)(2,1)} %bitcast.105) | data formatting | bytes 9437184
  55.3 0.9 convolution_bitcast_fusion.1
  56.2 0.9 convolution_bitcast_fusion
  57.2 1.1 pad_maximum_fusion
  59.1 0.2 fusion.15
  59.6 17.1 %reduce-scatter.2.cloned.1.call-done = f32[32,2,2304]{2,0,1:T(8,128)} async-done(((f32[64,2,2304]{2,0,1:T(8,128)}), f32[32,2,2304]{2,0,1:T(8,128)}) %reduce-scatter.2.cloned.1.call-update) | async-done | bytes 589840 | tf_op jit(solution)/shard_map/reduce_scatter | solution.py:50
  76.7 1.1 convert_element_type.32
  77.8 0.9 copy.77
  78.7 5.6 %all-to-all-start = ((bf16[32,2,2,1152]{3,2,1,0:T(2,128)(2,1)}), bf16[32,2,2,1152]{3,2,1,0:T(2,128)(2,1)S(1)}, u32[]{:S(2)}, u32[]{:S(2)}) async-start(bf16[32,2,2,1152]{3,2,1,0:T(2,128)(2,1)} %copy.77), calls=%async_computation.1 | async-start | bytes 589824 | tf_op jit(solution)/shard_map/all_to_all | solution.py:52
  84.4 0.1 maximum_bitcast_fusion.3
  84.5 0.1 maximum_bitcast_fusion
  84.7 10.2 %all-to-all-done = bf16[32,2,2,1152]{3,2,1,0:T(2,128)(2,1)S(1)} async-done(((bf16[32,2,2,1152]{3,2,1,0:T(2,128)(2,1)}), bf16[32,2,2,1152]{3,2,1,0:T(2,128)(2,1)S(1)}, u32[]{:S(2)}, u32[]{:S(2)}) %all-to-all-start) | async-done | bytes 294944 | tf_op jit(solution)/shard_map/all_to_all | solution.py:52
  94.9 0.2 copy.97
  95.1 3.0 %reshape.60 = bf16[2,2,32,32,36,1]{4,3,1,2,0,5:T(8,128)(2,1)S(1)} reshape(bf16[2,2,16,2,1152]{4,1,3,2,0:T(2,128)(2,1)S(1)} %copy.97) | data formatting | bytes 589824 | tf_op jit(solution)/shard_map/reshape | solution.py:22
  98.1 0.5 fusion
  98.6 0.5 fusion.1
  99.1 0.5 convolution_bitcast_fusion.2
  99.6 1.2 %copy.83 = f32[2,2,32,32,36]{4,3,2,1,0:T(8,128)S(1)} copy(f32[2,2,32,32,36]{4,2,3,1,0:T(8,128)S(1)} %convolution_bitcast_fusion.2) | data formatting | bytes 1179648 | tf_op jit(solution)/shard_map/qcmju,qcmdi->qdiju/dot_general | solution.py:35
  100.8 2.4 %reshape.52 = f32[2,2,32,1152]{3,2,1,0:T(8,128)} reshape(f32[2,2,32,32,36]{4,3,2,1,0:T(8,128)S(1)} %copy.83) | data formatting | bytes 1179648 | tf_op jit(solution)/shard_map/reshape | solution.py:36
  (22 shorter events, 0.6 us)
Async XLA Ops:
  6.5 52.5 %copy-start = (bf16[8,2,32,32]{3,2,1,0:T(8,128)(2,1)S(1)}, bf16[8,2,32,32]{3,2,1,0:T(8,128)(2,1)}, u32[]{:S(2)}) copy-start(bf16[8,2,32,32]{3,2,1,0:T(8,128)(2,1)} %param.11) | copy-start | bytes 98308
  6.5 70.1 %reduce-scatter.2.cloned.1.call-start = ((), (), s32[]{:S(2)}) async-start(), calls=%async_computation.2 | async-start | bytes 1769472 | tf_op jit(solution)/shard_map/reduce_scatter | solution.py:50
  57.1 1.1 %copy-start.1 = (bf16[2,2,36,36]{3,1,2,0:T(2,128)(2,1)S(1)}, bf16[2,2,36,36]{3,1,2,0:T(2,128)(2,1)}, u32[]{:S(2)}) copy-start(bf16[2,2,36,36]{3,1,2,0:T(2,128)(2,1)} %param.13) | copy-start | bytes 31108
  57.2 2.2 %copy-start.2 = (bf16[2,2,32,32]{3,2,1,0:T(8,128)(2,1)S(1)}, bf16[2,2,32,32]{3,2,1,0:T(8,128)(2,1)}, u32[]{:S(2)}) copy-start(bf16[2,2,32,32]{3,2,1,0:T(8,128)(2,1)} %param.12) | copy-start | bytes 24580
  78.7 16.2 %all-to-all-start = ((bf16[32,2,2,1152]{3,2,1,0:T(2,128)(2,1)}), bf16[32,2,2,1152]{3,2,1,0:T(2,128)(2,1)S(1)}, u32[]{:S(2)}, u32[]{:S(2)}) async-start(bf16[32,2,2,1152]{3,2,1,0:T(2,128)(2,1)} %copy.77), calls=%async_computation.1 | async-start | bytes 589824 | tf_op jit(solution)/shard_map/all_to_all | solution.py:52
Sparse Core Ops, SparseCore 0:
  58.4 18.1 reduce-scatter.1
